TPU v7x, 32 devices: a whole 2x2x4 slice. The times are simulated.
32 devices in a mesh: row: 8 (over z, x), col: 4 (over y, core).
Axes of the slice: x: 2, y: 2, z: 4, core: 2. Of those that a mesh axis runs over, the one named last changes fastest.
Arguments:
- panel_block: float32 [20480, 512], P('row', 'col'), may hold values from -12 to 12
- trailing: float32 [20480, 20480], P('row', 'col'), may hold values from -6 to 6
Outputs:
- updated: float32 [20480, 20480], P('row', 'col')
All inputs are finite; a program needn't handle non-finite values.
Results may differ from a plain program's by a relative error of at most 0.0003.
Values sent between devices are 32-bit elements; how exact they have to be, the bound alone decides.
No kernel may reach another device: no remote copies, remote signals or barrier semaphores. Data moves between devices by JAX's collectives and lax.ppermute only.
A program may use at most 192 MiB of HBM per device.

v0:
```python
import jax
import jax.numpy as jnp
from jax import lax
from jax.sharding import PartitionSpec as P

N = 20480


def on_device(panel_block, trailing):
    local_rows = panel_block.shape[0]
    local_width = panel_block.shape[1]
    rows_count = lax.axis_size("row")
    cols_count = lax.axis_size("col")
    copies = rows_count // cols_count
    row_owner = lax.axis_index("row")
    col_owner = lax.axis_index("col")
    mc_rows = lax.all_gather(panel_block, "col", axis=1, tiled=True)
    squares = lax.psum(jnp.sum(mc_rows * mc_rows), "row")
    column_block = lax.all_gather(panel_block, "row", axis=0, tiled=True)
    shaped = column_block.reshape(copies, cols_count, local_rows, local_width)
    moved = lax.all_to_all(shaped, "col", split_axis=1, concat_axis=3, tiled=True)
    stacked = moved.reshape(copies, local_rows, mc_rows.shape[1])
    mr_rows = jnp.transpose(stacked, (1, 0, 2)).reshape(copies * local_rows, stacked.shape[2])
    update = lax.dot_general(
        mc_rows,
        mr_rows,
        (((1,), (1,)), ((), ())),
        precision=lax.Precision.HIGHEST,
        preferred_element_type=jnp.float32,
    )
    row_index = jnp.arange(local_rows, dtype=jnp.int32) * rows_count + row_owner
    col_index = jnp.arange(mr_rows.shape[0], dtype=jnp.int32) * cols_count + col_owner
    lower_part = row_index[:, None] >= col_index[None, :]
    factor = 0.8 * jnp.sqrt(jnp.float32(N)) / jnp.sqrt(squares + 1e-06)
    return trailing - factor * jnp.where(lower_part, update, jnp.zeros_like(update))


def solution(mesh):
    in_specs = (P("row", "col"), P("row", "col"))
    out_specs = P("row", "col")
    return jax.shard_map(
        on_device, mesh=mesh, in_specs=in_specs, out_specs=out_specs, check_vma=False
    )
```

profile of v0, /device:TPU:0, one launch (start us, length us, event | category | flops | bytes accessed | tf_op | source)
XLA Modules:
  0.0 456.7 jit_solution(3020572873124051038)
XLA Ops:
  6.5 0.0 all-gather.5.cloned.1.call-start
  6.5 0.7 all-gather.5.cloned.1.call-update
  7.3 0.0 all-gather.3.cloned.1.call-start
  7.3 0.7 all-gather.3.cloned.1.call-update
  8.0 154.8 %all-gather.5.cloned.1.call-done = f32[20480,128]{1,0:T(8,128)} async-done(((f32[2560,128]{1,0:T(8,128)}), f32[20480,128]{1,0:T(8,128)}) %all-gather.5.cloned.1.call-update) | async-done | bytes 10485776 | tf_op jit(solution)/shard_map/all_gather | solution.py:19
  162.8 9.6 %copy.6 = f32[2,4,2560,128]{3,2,0,1:T(8,128)} copy(f32[2,4,2560,128]{3,2,1,0:T(8,128)} %bitcast.11) | data formatting | bytes 20971520 | tf_op jit(solution)/shard_map/reshape | solution.py:20
  172.4 6.0 %all-to-all-start = ((f32[2,4,2560,128]{3,2,0,1:T(8,128)}), f32[2,4,2560,128]{3,2,0,1:T(8,128)}, u32[]{:S(2)}, u32[]{:S(2)}) async-start(f32[2,4,2560,128]{3,2,0,1:T(8,128)} %copy.6), calls=%async_computation | async-start | bytes 20971520 | tf_op jit(solution)/shard_map/all_to_all | solution.py:21
  178.5 45.0 %all-gather.3.cloned.1.call-done = f32[2560,512]{1,0:T(8,128)} async-done(((f32[2560,128]{1,0:T(8,128)}), f32[2560,512]{1,0:T(8,128)}) %all-gather.3.cloned.1.call-update) | async-done | bytes 5242896 | tf_op jit(solution)/shard_map/all_gather | solution.py:17
  223.4 4.5 multiply_reduce_fusion
  227.9 25.2 %psum.7 = f32[]{:T(128)} all-reduce(f32[]{:T(128)} %multiply_reduce_fusion), channel_id=1, replica_groups=mesh['row'=8,'col'=4] {'row'}, use_global_device_ids=true, to_apply=%region_1.0 | all-reduce | flops 1 | bytes 8 | tf_op jit(solution)/shard_map/psum | solution.py:18
  253.8 60.0 %all-to-all-done = f32[2,4,2560,128]{3,2,0,1:T(8,128)} async-done(((f32[2,4,2560,128]{3,2,0,1:T(8,128)}), f32[2,4,2560,128]{3,2,0,1:T(8,128)}, u32[]{:S(2)}, u32[]{:S(2)}) %all-to-all-start) | async-done | bytes 10485792 | tf_op jit(solution)/shard_map/all_to_all | solution.py:21
  313.8 11.4 %copy.7 = f32[2,4,2560,128]{2,3,1,0:T(8,128)} copy(f32[2,4,2560,128]{3,2,0,1:T(8,128)} %all-to-all-done) | data formatting | bytes 20971520 | tf_op jit(solution)/shard_map/all_to_all | solution.py:21
  325.2 16.1 %copy.8 = f32[2560,2,512]{2,1,0:T(2,128)} copy(f32[2560,2,512]{0,2,1:T(8,128)} %bitcast.10) | data formatting | bytes 20971520 | tf_op jit(solution)/shard_map/transpose | solution.py:23
  341.3 13.3 %reshape.22 = f32[5120,512]{1,0:T(8,128)} reshape(f32[2560,2,512]{2,1,0:T(2,128)} %copy.8) | data formatting | bytes 20971520 | tf_op jit(solution)/shard_map/reshape | solution.py:23
  354.5 95.4 %multiply_subtract_fusion = f32[2560,5120]{1,0:T(8,128)} fusion(f32[2560,5120]{1,0:T(8,128)} %param.3, f32[2560,512]{1,0:T(8,128)} %all-gather.3.cloned.1.call-done, f32[5120,512]{1,0:T(8,128)} %reshape.22, s32[5120]{0:T(1024)S(1)} %multiply_add_fusion, f32[]{:T(128)S(6)} %div.3, s32[2560]{0:T(1024)S(1)} %multiply_add_fusion.1), kind=kOutput, calls=%fused_computation | convolution fusion | flops 80583065600 | bytes 120616960 | tf_op jit(solution)/shard_map/dot_general | solution.py:24
  (2 shorter events, 0.0 us)
Async XLA Ops:
  6.5 156.2 %all-gather.5.cloned.1.call-start = ((), (), s32[]{:S(2)}) async-start(), calls=%async_computation.2 | async-start | bytes 11796480 | tf_op jit(solution)/shard_map/all_gather | solution.py:19
  7.3 216.2 %all-gather.3.cloned.1.call-start = ((), (), s32[]{:S(2)}) async-start(), calls=%async_computation.1 | async-start | bytes 6553600 | tf_op jit(solution)/shard_map/all_gather | solution.py:17
  172.4 141.4 %all-to-all-start = ((f32[2,4,2560,128]{3,2,0,1:T(8,128)}), f32[2,4,2560,128]{3,2,0,1:T(8,128)}, u32[]{:S(2)}, u32[]{:S(2)}) async-start(f32[2,4,2560,128]{3,2,0,1:T(8,128)} %copy.6), calls=%async_computation | async-start | bytes 20971520 | tf_op jit(solution)/shard_map/all_to_all | solution.py:21
Sparse Core Ops, SparseCore 0:
  9.5 153.2 all-gather.4
  164.3 59.0 all-gather.2
where the time goes:
time: 458 us; the launch traced here: 457 us
  waiting for transfers between devices  261 us (57%)
  matrix products  95.4 us (21%)
  local copies, waits for them, and re-layouts  50.4 us (11%)
  blocking collectives  25.2 us (6%)
  between operations  14.1 us (3%)
  starting transfers between devices  6.08 us (1%)
    all_gather x1, waiting for transfers between devices, on_device(): column_block = lax.all_gather(panel_block, 'row', axis=0, tiled=True)  155 us
    dot_general x1, matrix products, on_device(): lax.dot_general(mc_rows, mr_rows, (((1,), (1,)), ((), ())), precision=lax...  95.4 us
    all_to_all x1, waiting for transfers between devices, on_device(): lax.all_to_all(shaped, 'col', split_axis=1, concat_axis=3, tiled=True)  60 us
    all_gather x1, waiting for transfers between devices, on_device(): mc_rows = lax.all_gather(panel_block, 'col', axis=1, tiled=True)  45 us
    psum x1, blocking collectives, on_device(): squares = lax.psum(jnp.sum(mc_rows * mc_rows), 'row')  25.2 us
    transpose x1, local copies, waits for them, and re-layouts, on_device(): jnp.transpose(stacked, (1, 0, 2))  16.1 us
    reshape x1, local copies, waits for them, and re-layouts, on_device(): jnp.transpose(stacked, (1, 0, 2))  13.3 us
    all_to_all x1, local copies, waits for them, and re-layouts, on_device(): lax.all_to_all(shaped, 'col', split_axis=1, concat_axis=3, tiled=True)  11.4 us
  transfers between devices with their start and end apart: 3, of which 3 were waited for; matrix products, arithmetic and copies ran while one was open for 3% of the time, Pallas kernels for 0%

commit v1 on v0

v1 whole, which is shorter than its diff:
```python
import jax
import jax.numpy as jnp
from jax import lax
from jax.experimental import pallas as pl
from jax.experimental.pallas import tpu as pltpu
from jax.sharding import PartitionSpec as P

SLABS = 4
TILES_PER_SLAB = 2


def split(x):
    hi = x.astype(jnp.bfloat16)
    lo = (x - hi.astype(jnp.float32)).astype(jnp.bfloat16)
    return hi, lo


def copy_upper(trailing, tile_rows, slab_cols):
    tiles = [(t, q) for q in range(1, SLABS) for t in range(TILES_PER_SLAB * q)]
    rows = jnp.array([t for t, _ in tiles], jnp.int32)
    cols = jnp.array([q for _, q in tiles], jnp.int32)

    def body(rows_ref, cols_ref, x_ref, o_ref):
        o_ref[...] = x_ref[...]

    spec = pl.BlockSpec((tile_rows, slab_cols), lambda n, rows, cols: (rows[n], cols[n]))
    return pl.pallas_call(
        body,
        grid_spec=pltpu.PrefetchScalarGridSpec(
            num_scalar_prefetch=2, grid=(len(tiles),), in_specs=[spec], out_specs=spec
        ),
        out_shape=jax.ShapeDtypeStruct(trailing.shape, trailing.dtype),
        name="copy_upper",
    )(rows, cols, trailing)


def update_slab(slab, where_am_i, factor, mine, gathered, trailing, out, rows_count, cols_count, copies):
    local_rows, local_cols = trailing.shape
    width = mine[0].shape[1]
    depth = width * cols_count
    slab_cols = local_cols // SLABS
    chunk = slab_cols // copies
    row_tiles = SLABS * TILES_PER_SLAB
    tile_rows = local_rows // row_tiles
    first = slab * TILES_PER_SLAB
    strided = width % 128 == 0
    if not strided:
        mixed = gathered.reshape(copies, cols_count, chunk, width)
        gathered = jnp.transpose(mixed, (1, 2, 0, 3)).reshape(cols_count, slab_cols, width)

    def body(place_ref, factor_ref, *refs):
        mine_refs = refs[:cols_count]
        g_ref, c_ref, _, o_ref, mixed_ref, b_ref, a_ref = refs[cols_count:]
        step = pl.program_id(0)
        row_owner = place_ref[0]
        col_owner = place_ref[1]

        @pl.when(step == 0)
        def _():
            for m in range(cols_count):
                source = col_owner ^ m
                if strided:
                    for s in range(copies):
                        mixed_ref[pl.ds(s, chunk, stride=copies), :] = g_ref[s * cols_count + source]
                    hi, lo = split(mixed_ref[...])
                else:
                    hi, lo = split(g_ref[source])
                b_ref[:, m * width:(m + 1) * width] = hi
                b_ref[:, depth + m * width:depth + (m + 1) * width] = lo
                b_ref[:, 2 * depth + m * width:2 * depth + (m + 1) * width] = hi

        for m in range(cols_count):
            hi, lo = split(mine_refs[m][...])
            a_ref[:, m * width:(m + 1) * width] = hi
            a_ref[:, depth + m * width:depth + (m + 1) * width] = hi
            a_ref[:, 2 * depth + m * width:2 * depth + (m + 1) * width] = lo
        product = lax.dot_general(
            a_ref[...], b_ref[...], (((1,), (1,)), ((), ())), preferred_element_type=jnp.float32
        )
        row = lax.broadcasted_iota(jnp.int32, (tile_rows, 1), 0) + (first + step) * tile_rows
        col = lax.broadcasted_iota(jnp.int32, (1, slab_cols), 1) + slab * slab_cols
        lower = row * rows_count + row_owner >= col * cols_count + col_owner
        o_ref[...] = c_ref[...] - jnp.where(lower, factor_ref[0] * product, 0.0)

    mine_spec = pl.BlockSpec((tile_rows, width), lambda n: (first + n, 0))
    tile_spec = pl.BlockSpec((tile_rows, slab_cols), lambda n: (first + n, slab))
    return pl.pallas_call(
        body,
        grid=(row_tiles - first,),
        in_specs=[
            pl.BlockSpec(memory_space=pltpu.SMEM),
            pl.BlockSpec(memory_space=pltpu.SMEM),
            *[mine_spec] * cols_count,
            pl.BlockSpec(gathered.shape, lambda n: (0, 0, 0)),
            tile_spec,
            pl.BlockSpec(memory_space=pl.ANY),
        ],
        out_specs=tile_spec,
        out_shape=jax.ShapeDtypeStruct(trailing.shape, trailing.dtype),
        scratch_shapes=[
            pltpu.VMEM((slab_cols, width), jnp.float32),
            pltpu.VMEM((slab_cols, 3 * depth), jnp.bfloat16),
            pltpu.VMEM((tile_rows, 3 * depth), jnp.bfloat16),
        ],
        input_output_aliases={cols_count + 4: 0},
        name=f"update_slab_{slab}",
    )(where_am_i, factor, *mine, gathered, trailing, out)


def on_device(panel_block, trailing):
    local_rows, width = panel_block.shape
    local_cols = trailing.shape[1]
    rows_count = lax.axis_size("row")
    cols_count = lax.axis_size("col")
    copies = rows_count // cols_count
    order = local_rows * rows_count
    row_owner = lax.axis_index("row")
    col_owner = lax.axis_index("col")
    chunk = local_rows // SLABS

    moves = []
    for r in range(rows_count):
        for c in range(cols_count):
            to = ((r // cols_count) * cols_count + c) * cols_count + r % cols_count
            moves.append((r * cols_count + c, to))
    moved = [
        lax.ppermute(panel_block[q * chunk:(q + 1) * chunk], ("row", "col"), moves)
        for q in range(SLABS)
    ]
    mine = {0: panel_block}
    bit = cols_count // 2
    while bit:
        pairs = [(c, c ^ bit) for c in range(cols_count)]
        for m in list(mine):
            mine[m ^ bit] = lax.ppermute(mine[m], "col", pairs)
        bit //= 2
    mine = [mine[m] for m in range(cols_count)]

    squares = lax.psum(jnp.sum(panel_block * panel_block), ("row", "col"))
    factor = 0.8 * jnp.sqrt(jnp.float32(order)) / jnp.sqrt(squares + 1e-06)
    where_am_i = jnp.stack([row_owner, col_owner]).astype(jnp.int32)

    out = copy_upper(trailing, local_rows // (SLABS * TILES_PER_SLAB), local_cols // SLABS)
    for q in range(SLABS):
        gathered = lax.all_gather(moved[q], "row", axis=0, tiled=False)
        out = update_slab(
            q, where_am_i, factor.reshape(1), mine, gathered, trailing, out, rows_count, cols_count, copies
        )
    return out


def solution(mesh):
    in_specs = (P("row", "col"), P("row", "col"))
    out_specs = P("row", "col")
    return jax.shard_map(
        on_device, mesh=mesh, in_specs=in_specs, out_specs=out_specs, check_vma=False
    )
```

time: 458 us -> 269 us (0.59)
  waiting for transfers between devices: 261 us -> 56.9 us
  matrix products: 95.4 us -> 0 us
  Pallas kernels: 0 us -> 73.7 us
  starting transfers between devices: 6.08 us -> 75.5 us
  local copies, waits for them, and re-layouts: 50.4 us -> 4.38 us
  blocking collectives: 25.2 us -> 41.7 us
    all_gather x2 -> x4, waiting for transfers between devices: 200 us -> 29.6 us  [on_device(): gathered = lax.all_gather(moved[q], 'row', axis=0, tiled=False)]
    dot_general x1 -> x0, matrix products: 95.4 us -> none  [on_device(): lax.dot_general(mc_rows, mr_rows, (((1,), (1,)), ((), ())), precision=lax...]
    ppermute x0 -> x7, starting transfers between devices: none -> 75.4 us  [the longest x3 72.7 us: on_device(): mine[m ^ bit] = lax.ppermute(mine[m], 'col', pairs)]
    pallas_call x0 -> x5, Pallas kernels: none -> 73.7 us  [the longest x4 55.6 us: update_slab(): pl.pallas_call(body, grid=(row_tiles - first,), in_specs=[pl.BlockSpec(me...]
    all_to_all x1 -> x0, waiting for transfers between devices: 60 us -> none  [on_device(): lax.all_to_all(shaped, 'col', split_axis=1, concat_axis=3, tiled=True)]
    ppermute x0 -> x7, waiting for transfers between devices: none -> 27.2 us  [the longest x3 27.2 us: on_device(): mine[m ^ bit] = lax.ppermute(mine[m], 'col', pairs)]
    reshape x2 -> x0, local copies, waits for them, and re-layouts: 22.9 us -> none  [the longest x1 13.3 us: on_device(): jnp.transpose(stacked, (1, 0, 2))]
    psum x1, blocking collectives: 25.2 us -> 41.7 us  [on_device(): squares = lax.psum(jnp.sum(panel_block * panel_block), ('row', 'col'))]
  transfers between devices with their start and end apart: 3 -> 11, of which waited for: 3 -> 2; matrix products, arithmetic and copies ran while one was open for 3% -> 1% of each run, Pallas kernels for 0% -> 25%
where the time goes in v1:
time: 269 us; the launch traced here: 268 us
  starting transfers between devices  75.5 us (28%)
  Pallas kernels  73.7 us (27%)
  waiting for transfers between devices  56.9 us (21%)
  blocking collectives  41.7 us (16%)
  between operations  13.9 us (5%)
  local copies, waits for them, and re-layouts  4.38 us (2%)
    ppermute x3, starting transfers between devices, on_device(): mine[m ^ bit] = lax.ppermute(mine[m], 'col', pairs)  72.7 us
    pallas_call x4, Pallas kernels, update_slab(): pl.pallas_call(body, grid=(row_tiles - first,), in_specs=[pl.BlockSpec(me...  55.6 us
    psum x1, blocking collectives, on_device(): squares = lax.psum(jnp.sum(panel_block * panel_block), ('row', 'col'))  41.7 us
    all_gather x4, waiting for transfers between devices, on_device(): gathered = lax.all_gather(moved[q], 'row', axis=0, tiled=False)  29.6 us
    ppermute x3, waiting for transfers between devices, on_device(): mine[m ^ bit] = lax.ppermute(mine[m], 'col', pairs)  27.2 us
    pallas_call x1, Pallas kernels, copy_upper(): pl.pallas_call(body, grid_spec=pltpu.PrefetchScalarGridSpec(num_scalar_pr...  18.1 us
  transfers between devices with their start and end apart: 11, of which 2 were waited for; matrix products, arithmetic and copies ran while one was open for 1% of the time, Pallas kernels for 25%

profile of v1, /device:TPU:0, one launch (start us, length us, event | category | flops | bytes accessed | tf_op | source)
XLA Modules:
  0.0 267.7 jit_solution(1208316667793595370)
XLA Ops:
  6.5 0.0 copy-start
  6.5 0.0 all-gather.15.cloned.1.call-start
  6.5 1.5 fusion
  8.0 0.7 collective-permute-start.6
  8.7 0.0 collective-permute-done.6
  8.7 0.0 copy-start.2
  8.7 0.7 copy-done.2
  9.4 0.0 all-gather.15.cloned.1.call-update
  9.5 0.0 all-gather.13.cloned.1.call-start
  9.5 0.7 collective-permute-start.5
  10.2 0.0 collective-permute-done.5
  10.2 0.0 copy-start.3
  10.2 0.7 copy-done.3
  11.0 0.0 all-gather.13.cloned.1.call-update
  11.0 0.0 all-gather.11.cloned.1.call-start
  11.0 0.7 collective-permute-start.4
  11.7 0.0 collective-permute-done.4
  11.7 0.0 copy-start.4
  11.7 0.7 copy-done.4
  12.4 0.0 all-gather.11.cloned.1.call-update
  12.5 0.0 all-gather.9.cloned.1.call-start
  12.5 0.7 collective-permute-start.3
  13.2 0.0 collective-permute-done.3
  13.2 0.0 copy-start.5
  13.2 0.7 copy-done.5
  14.0 0.0 all-gather.9.cloned.1.call-update
  14.0 0.0 copy-done
  14.0 72.7 %collective-permute-start.1 = (f32[2560,128]{1,0:T(8,128)S(1)}, f32[2560,128]{1,0:T(8,128)S(1)}, u32[]{:S(2)}, u32[]{:S(2)}) collective-permute-start(f32[2560,128]{1,0:T(8,128)S(1)} %copy-done), channel_id=1, source_target_pairs={{0,2},{1,3},{2,0},{3,1},{4,6},{5,7},{6,4},{7,5},{8,10},{9,11},{10,... | collective-permute-start | bytes 3932168 | tf_op jit(solution)/shard_map/ppermute | solution.py:135
  86.7 0.0 collective-permute-start
  86.7 27.2 %collective-permute-done.1.refs_2_ = f32[2560,128]{1,0:T(8,128)S(1)} collective-permute-done((f32[2560,128]{1,0:T(8,128)S(1)}, f32[2560,128]{1,0:T(8,128)S(1)}, u32[]{:S(2)}, u32[]{:S(2)}) %collective-permute-start.1) | collective-permute-done | bytes 1310752 | tf_op jit(solution)/shard_map/ppermute | solution.py:135
  113.9 0.0 copy-start.1
  113.9 0.0 collective-permute-start.2
  113.9 0.9 multiply_reduce_fusion
  114.8 41.7 %psum.7 = f32[]{:T(128)} all-reduce(f32[]{:T(128)} %multiply_reduce_fusion), channel_id=1, replica_groups=mesh['row'=8,'col'=4] {'row','col'}, use_global_device_ids=true, to_apply=%region_1.0 | all-reduce | flops 1 | bytes 8 | tf_op jit(solution)/shard_map/psum | solution.py:139
  157.2 18.1 %copy_upper.1.refs_6_ = f32[2560,5120]{1,0:T(8,128)} custom-call(s32[12]{0:T(128)} %constant.19.clone.rows_ref, s32[12]{0:T(128)} %constant.20.clone.cols_ref, f32[2560,5120]{1,0:T(8,128)} %refs_5_.7), custom_call_target="tpu_custom_call" | custom-call | tf_op jit(solution)/shard_map/copy_upper/pallas_call | solution.py:27
  175.3 0.0 copy-done.1
  175.3 0.6 pad_add_fusion.place_ref
  175.9 0.0 collective-permute-done.refs_1_
  175.9 0.0 collective-permute-done.2.refs_3_
  175.9 0.0 all-gather.15.cloned.1.call-done
  175.9 19.8 %update_slab_0.1.refs_6_ = f32[2560,5120]{1,0:T(8,128)} custom-call(s32[2]{0:T(128)} %pad_add_fusion.place_ref, f32[1]{0:T(128)} %bitcast.2.factor_ref, f32[2560,128]{1,0:T(8,128)} %refs_0_.7, f32[2560,128]{1,0:T(8,128)} %collective-permute-done.refs_1_, f32[2560,128]{1,0:T(8,128)} %copy-done.1, ...), custom_call_target="tpu_custom_call", output_to_operand_aliasing={{}: (8, {})} | custom-call | tf_op jit(solution)/shard_map/update_slab_0/pallas_call | solution.py:87
  195.7 0.0 all-gather.13.cloned.1.call-done
  195.7 15.8 %update_slab_1.1.refs_6_ = f32[2560,5120]{1,0:T(8,128)} custom-call(s32[2]{0:T(128)} %pad_add_fusion.place_ref, f32[1]{0:T(128)} %bitcast.2.factor_ref, f32[2560,128]{1,0:T(8,128)} %refs_0_.7, f32[2560,128]{1,0:T(8,128)} %collective-permute-done.refs_1_, f32[2560,128]{1,0:T(8,128)} %copy-done.1, ...), custom_call_target="tpu_custom_call", output_to_operand_aliasing={{}: (8, {})} | custom-call | tf_op jit(solution)/shard_map/update_slab_1/pallas_call | solution.py:87
  211.5 0.0 all-gather.11.cloned.1.call-done
  211.5 12.0 %update_slab_2.1.refs_6_ = f32[2560,5120]{1,0:T(8,128)} custom-call(s32[2]{0:T(128)} %pad_add_fusion.place_ref, f32[1]{0:T(128)} %bitcast.2.factor_ref, f32[2560,128]{1,0:T(8,128)} %refs_0_.7, f32[2560,128]{1,0:T(8,128)} %collective-permute-done.refs_1_, f32[2560,128]{1,0:T(8,128)} %copy-done.1, ...), custom_call_target="tpu_custom_call", output_to_operand_aliasing={{}: (8, {})} | custom-call | tf_op jit(solution)/shard_map/update_slab_2/pallas_call | solution.py:87
  223.5 29.6 %all-gather.9.cloned.1.call-done = f32[5120,128]{1,0:T(8,128)} async-done(((f32[640,128]{1,0:T(8,128)}), f32[5120,128]{1,0:T(8,128)}) %all-gather.9.cloned.1.call-update) | async-done | bytes 2621456 | tf_op jit(solution)/shard_map/all_gather | solution.py:145
  253.1 8.0 %update_slab_3.1 = f32[2560,5120]{1,0:T(8,128)} custom-call(s32[2]{0:T(128)} %pad_add_fusion.place_ref, f32[1]{0:T(128)} %bitcast.2.factor_ref, f32[2560,128]{1,0:T(8,128)} %refs_0_.7, f32[2560,128]{1,0:T(8,128)} %collective-permute-done.refs_1_, f32[2560,128]{1,0:T(8,128)} %copy-done.1, ...), custom_call_target="tpu_custom_call", output_to_operand_aliasing={{}: (8, {})} | custom-call | tf_op jit(solution)/shard_map/update_slab_3/pallas_call | solution.py:87
Async XLA Ops:
  6.5 7.5 %copy-start = (f32[2560,128]{1,0:T(8,128)S(1)}, f32[2560,128]{1,0:T(8,128)}, u32[]{:S(2)}) copy-start(f32[2560,128]{1,0:T(8,128)} %refs_0_.7) | copy-start | bytes 3932164
  6.5 169.3 %all-gather.15.cloned.1.call-start = ((), (), s32[]{:S(2)}) async-start(), calls=%async_computation.3 | async-start | bytes 2949120 | tf_op jit(solution)/shard_map/all_gather | solution.py:145
  8.0 0.7 collective-permute-start.6
  8.7 0.7 copy-start.2
  9.5 186.2 %all-gather.13.cloned.1.call-start = ((), (), s32[]{:S(2)}) async-start(), calls=%async_computation.2 | async-start | bytes 2949120 | tf_op jit(solution)/shard_map/all_gather | solution.py:145
  9.5 0.7 collective-permute-start.5
  10.2 0.7 copy-start.3
  11.0 200.5 %all-gather.11.cloned.1.call-start = ((), (), s32[]{:S(2)}) async-start(), calls=%async_computation.1 | async-start | bytes 2949120 | tf_op jit(solution)/shard_map/all_gather | solution.py:145
  11.0 0.7 collective-permute-start.4
  11.7 0.7 copy-start.4
  12.5 240.6 %all-gather.9.cloned.1.call-start = ((), (), s32[]{:S(2)}) async-start(), calls=%async_computation | async-start | bytes 2949120 | tf_op jit(solution)/shard_map/all_gather | solution.py:145
  12.5 0.7 collective-permute-start.3
  13.2 0.8 copy-start.5
  14.0 99.9 %collective-permute-start.1 = (f32[2560,128]{1,0:T(8,128)S(1)}, f32[2560,128]{1,0:T(8,128)S(1)}, u32[]{:S(2)}, u32[]{:S(2)}) collective-permute-start(f32[2560,128]{1,0:T(8,128)S(1)} %copy-done), channel_id=1, source_target_pairs={{0,2},{1,3},{2,0},{3,1},{4,6},{5,7},{6,4},{7,5},{8,10},{9,11},{10,... | collective-permute-start | bytes 3932168 | tf_op jit(solution)/shard_map/ppermute | solution.py:135
  86.7 89.2 %collective-permute-start = (f32[2560,128]{1,0:T(8,128)S(1)}, f32[2560,128]{1,0:T(8,128)}, u32[]{:S(2)}, u32[]{:S(2)}) collective-permute-start(f32[2560,128]{1,0:T(8,128)S(1)} %copy-done), channel_id=1, source_target_pairs={{0,1},{1,0},{2,3},{3,2},{4,5},{5,4},{6,7},{7,6},{8,9},{9,8},{10,11... | collective-permute-start | bytes 3932168 | tf_op jit(solution)/shard_map/ppermute | solution.py:135
  113.9 61.4 %copy-start.1 = (f32[2560,128]{1,0:T(8,128)}, f32[2560,128]{1,0:T(8,128)S(1)}, u32[]{:S(2)}) copy-start(f32[2560,128]{1,0:T(8,128)S(1)} %collective-permute-done.1.refs_2_) | copy-start | bytes 3932164
  113.9 62.0 %collective-permute-start.2 = (f32[2560,128]{1,0:T(8,128)S(1)}, f32[2560,128]{1,0:T(8,128)}, u32[]{:S(2)}, u32[]{:S(2)}) collective-permute-start(f32[2560,128]{1,0:T(8,128)S(1)} %collective-permute-done.1.refs_2_), channel_id=1, source_target_pairs={{0,1},{1,0},{2,3},{3,2},{4,5},{5,4},{6,7},{7,6},{8,9},{9,8},{10,11... | collective-permute-start | bytes 3932168 | tf_op jit(solution)/shard_map/ppermute | solution.py:135
Sparse Core Ops, SparseCore 0:
  9.6 75.3 all-gather.14
  87.2 55.5 all-gather.12
  145.0 52.9 all-gather.10
  200.1 52.9 all-gather.8
